TPU v7x, 32 devices: a whole 2x2x4 slice. The times are simulated.
32 devices in a mesh: pair: 4 (over y, x), virt: 8 (over z, core).
Axes of the slice: x: 2, y: 2, z: 4, core: 2. Of those that a mesh axis runs over, the one named last changes fastest.
Arguments:
- density_row_blocks: bfloat16 [160, 128, 2744], P('pair', 'virt'), may hold values from -6 to 6
- vir_left: bfloat16 [128, 2744], P('virt'), may hold values from -0.046875 to 0.046875
- vir_right: bfloat16 [128, 2744], P('virt'), may hold values from -0.109375 to 0.109375
- orb_energy: bfloat16 [128], P('virt'), may hold values from 0.5 to 3
- state_energy: float32 [8], replicated, may hold values from -1 to -0.1
- bra_ket_states: int32 [160, 2], P('pair'), may hold values from 0 to 7
- row_block_starts: int32 [160], P('pair'), may hold values from 0 to 2616
Outputs:
- slot_couplings: float32 [160], P('pair')
- heff: float32 [8, 8], replicated
All inputs are finite; a program needn't handle non-finite values.
Results may differ from a plain program's by a relative error of at most 0.0003.
Values may be sent and summed in bfloat16 or wider, within the bound.
A program may use at most 64 MiB of HBM per device.

v0:
```python
import jax
import jax.numpy as jnp
from jax import lax
from jax.sharding import PartitionSpec as P


def local(
    density_row_blocks,
    vir_left,
    vir_right,
    orb_energy,
    state_energy,
    bra_ket_states,
    row_block_starts,
):
    slots, rows, ntrip = density_row_blocks.shape
    nstate = state_energy.shape[0]
    virt_index = lax.axis_index("virt")
    positions = (
        row_block_starts[:, None] + virt_index * rows + jnp.arange(rows, dtype=jnp.int32)[None, :]
    )
    positions = positions.reshape(slots * rows)
    flat_rdm = density_row_blocks.reshape(slots * rows, ntrip)
    states = jnp.arange(nstate, dtype=jnp.int32)
    first = (bra_ket_states[:, 0:1] == states[None, :]).astype(jnp.float32)
    second = (bra_ket_states[:, 1:2] == states[None, :]).astype(jnp.float32)
    shift = jnp.dot(first + second, state_energy, precision=lax.Precision.HIGHEST)
    columns = jnp.take(lax.all_gather(vir_left, "virt", axis=0, tiled=True), positions, axis=1)
    right_piece = lax.all_gather(vir_right, "virt", axis=0, tiled=True)
    count = right_piece.shape[0]
    contracted = lax.dot_general(
        right_piece, flat_rdm, (((1,), (1,)), ((), ())), preferred_element_type=jnp.float32
    )
    inverse = 1.0 / (
        lax.all_gather(orb_energy, "virt", axis=0, tiled=True).astype(jnp.float32)[:, None]
        - shift[None, :]
    )
    product = columns.astype(jnp.float32).reshape(count, slots, rows) * contracted.reshape(
        count, slots, rows
    )
    partial_sums = jnp.sum(jnp.sum(product, axis=2) * inverse, axis=0)
    couplings = lax.psum(partial_sums, "virt")
    local_sum = jnp.dot(first.T, couplings[:, None] * second, precision=lax.Precision.HIGHEST)
    collected = lax.all_gather(local_sum[None], "pair", axis=0, tiled=True)
    coupling_sum = jnp.sum(collected, axis=0)
    heff = jnp.diag(state_energy) + 0.5 * (coupling_sum + coupling_sum.T)
    return (couplings, heff)


def solution(mesh):
    placed = (
        P("pair", "virt", None),
        P("virt", None),
        P("virt", None),
        P("virt"),
        P(),
        P("pair", None),
        P("pair"),
    )
    return jax.shard_map(
        local, mesh=mesh, in_specs=placed, out_specs=(P("pair"), P()), check_vma=False
    )
```

profile of v0, /device:TPU:0, one launch (start us, length us, event | category | flops | bytes accessed | tf_op | source)
XLA Modules:
  0.0 82.9 jit_solution(17060475857912333870)
XLA Ops:
  0.6 0.7 broadcast_add_fusion
  1.3 0.1 copy.22
  1.4 0.1 add.74
  1.5 17.2 %all_gather.12 = bf16[128,2744]{1,0:T(8,128)(2,1)S(1)} all-gather(bf16[16,2744]{1,0:T(8,128)(2,1)} %param.8), channel_id=1, replica_groups=mesh['pair'=4,'virt'=8] {'virt'}, dimensions={0}, use_global_device_ids=true | all-gather | bytes 790272 | tf_op jit(solution)/shard_map/all_gather | solution.py:28
  18.8 0.4 copy.23
  19.1 2.0 %gather_fusion = bf16[640,128]{1,0:T(8,128)(2,1)S(1)} fusion(bf16[128,2744]{0,1:T(8,128)(2,1)S(1)} %copy.23, s32[1024]{0:T(1024)S(1)} %pad_clamp_fusion), kind=kCustom, calls=%fused_computation | custom fusion | bytes 330240 | tf_op jit(solution)/shard_map/jit(_take)/gather | solution.py:28
  21.1 0.0 copy-start.1
  21.2 0.0 copy-start.2
  21.2 0.0 copy-start.4
  21.2 0.0 copy-start.3
  21.2 15.5 %all_gather.13 = bf16[128,2744]{1,0:T(8,128)(2,1)S(1)} all-gather(bf16[16,2744]{1,0:T(8,128)(2,1)S(1)} %copy-done), channel_id=1, replica_groups=mesh['pair'=4,'virt'=8] {'virt'}, dimensions={0}, use_global_device_ids=true | all-gather | bytes 790272 | tf_op jit(solution)/shard_map/all_gather | solution.py:29
  36.7 3.8 %fusion.5 = f32[128,40]{0,1:T(8,128)S(1)} fusion(bf16[40,16,2744]{2,1,0:T(8,128)(2,1)} %param.7, bf16[128,2744]{1,0:T(8,128)(2,1)S(1)} %all_gather.13, bf16[128,40,16]{0,2,1:T(8,128)(2,1)S(1)} %bitcast.24, pred[40,16]{0,1:T(8,128)(4,1)S(1)} %compare_and_fusion), kind=kOutput, calls=%fused_computation.4 | convolution fusion | flops 449899520 | bytes 4399744 | tf_op jit(solution)/shard_map/dot_general | solution.py:31
  40.5 0.0 copy-done.2
  40.5 0.2 convolution_bitcast_fusion
  40.7 0.6 dynamic-slice
  42.0 0.0 copy-done.3
  42.0 0.2 dynamic-update-slice
  42.2 17.7 %all-reduce = bf16[128]{0:T(256)(128)(2,1)S(1)} all-reduce(bf16[128]{0:T(256)(128)(2,1)S(1)} %dynamic-update-slice), channel_id=1, replica_groups=mesh['pair'=4,'virt'=8] {'virt'}, use_global_device_ids=true, to_apply=%add | all-reduce | flops 128 | bytes 512
  60.0 0.2 multiply_reduce_fusion
  60.1 13.6 %psum.7 = f32[40]{0:T(128)S(1)} all-reduce(f32[40]{0:T(128)S(1)} %multiply_reduce_fusion), channel_id=1, replica_groups=mesh['pair'=4,'virt'=8] {'virt'}, use_global_device_ids=true, to_apply=%region_2.3 | all-reduce | flops 40 | bytes 320 | tf_op jit(solution)/shard_map/psum | solution.py:42
  73.7 0.3 fusion.9
  74.0 8.2 %all-gather = f32[32,8]{1,0:T(8,128)S(1)} all-gather(f32[8,8]{1,0:T(8,128)S(1)} %fusion.9), channel_id=2, replica_groups=mesh['pair'=4,'virt'=8] {'pair'}, dimensions={0}, use_global_device_ids=true | all-gather | bytes 1280 | tf_op jit(solution)/shard_map/all_gather | solution.py:44
  82.2 0.1 copy.26
  82.3 0.7 fusion.21
  (14 shorter events, 0.1 us)
Async XLA Ops:
  0.6 20.6 %copy-start = (bf16[16,2744]{1,0:T(8,128)(2,1)S(1)}, bf16[16,2744]{1,0:T(8,128)(2,1)}, u32[]{:S(2)}) copy-start(bf16[16,2744]{1,0:T(8,128)(2,1)} %param.9) | copy-start | bytes 263428
  21.1 19.3 %copy-start.1 = (s32[40,2]{0,1:T(2,128)S(1)}, s32[40,2]{0,1:T(2,128)}, u32[]{:S(2)}) copy-start(s32[40,2]{0,1:T(2,128)} %param.12) | copy-start | bytes 964
  21.2 19.3 %copy-start.2 = (f32[8]{0:T(128)S(1)}, f32[8]{0:T(128)}, u32[]{:S(2)}) copy-start(f32[8]{0:T(128)} %param.11) | copy-start | bytes 100
  21.2 19.5 %copy-start.4 = (u32[32]{0:T(128)S(1)}, u32[32]{0:T(128)}, u32[]{:S(2)}) copy-start(u32[32]{0:T(128)} %constant.33) | copy-start | bytes 388
  21.2 20.8 %copy-start.3 = (bf16[16]{0:T(256)(128)(2,1)S(1)}, bf16[16]{0:T(256)(128)(2,1)}, u32[]{:S(2)}) copy-start(bf16[16]{0:T(256)(128)(2,1)} %param.10) | copy-start | bytes 100
  73.7 9.2 %copy-start.5 = (f32[40]{0:T(128)}, f32[40]{0:T(128)S(1)}, u32[]{:S(2)}) copy-start(f32[40]{0:T(128)S(1)} %psum.7) | copy-start | bytes 484
where the time goes:
time: 83.2 us; the launch traced here: 82.9 us
  blocking collectives  72.2 us (87%)
  matrix products  4.26 us (5%)
  local copies, waits for them, and re-layouts  3.48 us (4%)
  other arithmetic  1.59 us (2%)
  between operations  1.41 us (2%)
    unnamed x1, blocking collectives  17.7 us
    all_gather x1, blocking collectives, local(): lax.all_gather(vir_left, 'virt', axis=0, tiled=True)  17.2 us
    all_gather x1, blocking collectives, local(): right_piece = lax.all_gather(vir_right, 'virt', axis=0, tiled=True)  15.5 us
    psum x1, blocking collectives, local(): couplings = lax.psum(partial_sums, 'virt')  13.6 us
    all_gather x1, blocking collectives, local(): collected = lax.all_gather(local_sum[None], 'pair', axis=0, tiled=True)  8.18 us
    dot_general x1, matrix products, local(): lax.dot_general(right_piece, flat_rdm, (((1,), (1,)), ((), ())), preferre...  3.8 us
    gather x1, local copies, waits for them, and re-layouts, local(): jnp.take(lax.all_gather(vir_left, 'virt', axis=0, tiled=True), positions,...  1.99 us

commit v1 on v0

--- a/solution.py
+++ b/solution.py
@@ -39,7 +39,11 @@
         count, slots, rows
     )
     partial_sums = jnp.sum(jnp.sum(product, axis=2) * inverse, axis=0)
-    couplings = lax.psum(partial_sums, "virt")
+    couplings = partial_sums
+    for hop in (1, 2, 4):
+        couplings = couplings + lax.ppermute(
+            couplings, "virt", [(dev, dev ^ hop) for dev in range(8)]
+        )
     local_sum = jnp.dot(first.T, couplings[:, None] * second, precision=lax.Precision.HIGHEST)
     collected = lax.all_gather(local_sum[None], "pair", axis=0, tiled=True)
     coupling_sum = jnp.sum(collected, axis=0)

time: 83.2 us -> 81 us (0.974)
  blocking collectives: 72.2 us -> 58.8 us
  waiting for transfers between devices: 0 us -> 9.18 us
  local copies, waits for them, and re-layouts: 3.48 us -> 5.44 us
    psum x1 -> x0, blocking collectives: 13.6 us -> none  [local(): couplings = lax.psum(partial_sums, 'virt')]
    ppermute x0 -> x3, waiting for transfers between devices: none -> 9.18 us  [local(): lax.ppermute(couplings, 'virt', [(dev, dev ^ hop) for dev in range(8)])]
    unnamed x15 -> x7, local copies, waits for them, and re-layouts: 0.89 us -> 2.11 us
  transfers between devices with their start and end apart: 0 -> 3, of which waited for: 0 -> 3; matrix products, arithmetic and copies ran while one was open for 0% -> 0% of each run, Pallas kernels for 0% -> 0%
where the time goes in v1:
time: 81 us; the launch traced here: 80.7 us
  blocking collectives  58.8 us (73%)
  waiting for transfers between devices  9.18 us (11%)
  local copies, waits for them, and re-layouts  5.44 us (7%)
  matrix products  4.28 us (5%)
  other arithmetic  1.57 us (2%)
  between operations  1.36 us (2%)
    unnamed x1, blocking collectives  17.7 us
    all_gather x1, blocking collectives, local(): lax.all_gather(vir_left, 'virt', axis=0, tiled=True)  17.2 us
    all_gather x1, blocking collectives, local(): right_piece = lax.all_gather(vir_right, 'virt', axis=0, tiled=True)  15.7 us
    ppermute x3, waiting for transfers between devices, local(): lax.ppermute(couplings, 'virt', [(dev, dev ^ hop) for dev in range(8)])  9.18 us
    all_gather x1, blocking collectives, local(): collected = lax.all_gather(local_sum[None], 'pair', axis=0, tiled=True)  8.19 us
    dot_general x1, matrix products, local(): lax.dot_general(right_piece, flat_rdm, (((1,), (1,)), ((), ())), preferre...  3.82 us
    unnamed x7, local copies, waits for them, and re-layouts  2.11 us
    gather x1, local copies, waits for them, and re-layouts, local(): jnp.take(lax.all_gather(vir_left, 'virt', axis=0, tiled=True), positions,...  1.98 us
  transfers between devices with their start and end apart: 3, of which 3 were waited for; matrix products, arithmetic and copies ran while one was open for 0% of the time, Pallas kernels for 0%

profile of v1, /device:TPU:0, one launch (start us, length us, event | category | flops | bytes accessed | tf_op | source)
XLA Modules:
  0.0 80.7 jit_solution(3836860676254951525)
XLA Ops:
  0.6 0.7 broadcast_add_fusion
  1.3 0.1 copy.22
  1.4 0.1 add.81
  1.5 17.2 %all_gather.12 = bf16[128,2744]{1,0:T(8,128)(2,1)S(1)} all-gather(bf16[16,2744]{1,0:T(8,128)(2,1)} %param.8), channel_id=1, replica_groups=mesh['pair'=4,'virt'=8] {'virt'}, dimensions={0}, use_global_device_ids=true | all-gather | bytes 790272 | tf_op jit(solution)/shard_map/all_gather | solution.py:28
  18.8 0.4 copy.23
  19.1 15.7 %all_gather.13 = bf16[128,2744]{1,0:T(8,128)(2,1)S(1)} all-gather(bf16[16,2744]{1,0:T(8,128)(2,1)} %param.9), channel_id=1, replica_groups=mesh['pair'=4,'virt'=8] {'virt'}, dimensions={0}, use_global_device_ids=true | all-gather | bytes 790272 | tf_op jit(solution)/shard_map/all_gather | solution.py:29
  34.8 0.8 slice_bitcast_fusion.1
  35.5 1.2 %dynamic-slice = u32[1]{0:T(128)} dynamic-slice(u32[32]{0:T(128)} %constant.33, u32[]{:T(128)S(6)} %add.90), dynamic_slice_sizes={1} | dynamic-slice | bytes 12
  37.4 0.9 %dynamic-update-slice = bf16[128]{0:T(256)(128)(2,1)S(1)} dynamic-update-slice(bf16[128]{0:T(256)(128)(2,1)S(1)} %broadcast.43, bf16[16]{0:T(256)(128)(2,1)} %param.10, u32[]{:T(128)} %bitcast.3) | dynamic-update-slice | bytes 68
  38.3 17.7 %all-reduce = bf16[128]{0:T(256)(128)(2,1)S(1)} all-reduce(bf16[128]{0:T(256)(128)(2,1)S(1)} %dynamic-update-slice), channel_id=1, replica_groups=mesh['pair'=4,'virt'=8] {'virt'}, use_global_device_ids=true, to_apply=%add | all-reduce | flops 128 | bytes 512
  56.0 2.0 %gather_fusion = bf16[640,128]{1,0:T(8,128)(2,1)S(1)} fusion(bf16[128,2744]{0,1:T(8,128)(2,1)S(1)} %copy.23, s32[1024]{0:T(1024)S(1)} %pad_clamp_fusion), kind=kCustom, calls=%fused_computation | custom fusion | bytes 330240 | tf_op jit(solution)/shard_map/jit(_take)/gather | solution.py:28
  58.0 0.2 convolution_bitcast_fusion
  58.2 3.8 %fusion.5 = f32[128,40]{0,1:T(8,128)S(1)} fusion(bf16[40,16,2744]{2,1,0:T(8,128)(2,1)} %param.7, bf16[128,2744]{1,0:T(8,128)(2,1)S(1)} %all_gather.13, bf16[128,40,16]{0,2,1:T(8,128)(2,1)S(1)} %bitcast.24, pred[40,16]{0,1:T(8,128)(4,1)S(1)} %compare_and_fusion), kind=kOutput, calls=%fused_computation.4 | convolution fusion | flops 449899520 | bytes 4399744 | tf_op jit(solution)/shard_map/dot_general | solution.py:31
  62.1 0.2 multiply_reduce_fusion
  62.3 0.1 collective-permute-start
  62.3 1.1 %collective-permute-done = f32[40]{0:T(128)S(1)} collective-permute-done((f32[40]{0:T(128)S(1)}, f32[40]{0:T(128)S(1)}, u32[]{:S(2)}, u32[]{:S(2)}) %collective-permute-start) | collective-permute-done | bytes 192 | tf_op jit(solution)/shard_map/ppermute | solution.py:44
  63.5 0.0 collective-permute-start.1
  63.5 3.6 %collective-permute-done.1 = f32[40]{0:T(128)S(1)} collective-permute-done((f32[40]{0:T(128)S(1)}, f32[40]{0:T(128)S(1)}, u32[]{:S(2)}, u32[]{:S(2)}) %collective-permute-start.1) | collective-permute-done | bytes 192 | tf_op jit(solution)/shard_map/ppermute | solution.py:44
  67.1 0.0 collective-permute-start.2
  67.1 4.5 %collective-permute-done.2 = f32[40]{0:T(128)S(1)} collective-permute-done((f32[40]{0:T(128)S(1)}, f32[40]{0:T(128)S(1)}, u32[]{:S(2)}, u32[]{:S(2)}) %collective-permute-start.2) | collective-permute-done | bytes 192 | tf_op jit(solution)/shard_map/ppermute | solution.py:44
  71.5 0.3 fusion.9
  71.8 8.2 %all-gather = f32[32,8]{1,0:T(8,128)S(1)} all-gather(f32[8,8]{1,0:T(8,128)S(1)} %fusion.9), channel_id=2, replica_groups=mesh['pair'=4,'virt'=8] {'pair'}, dimensions={0}, use_global_device_ids=true | all-gather | bytes 1280 | tf_op jit(solution)/shard_map/all_gather | solution.py:48
  80.0 0.1 copy.26
  80.1 0.7 fusion.21
  (14 shorter events, 0.1 us)
Async XLA Ops:
  0.6 57.4 %copy-start = (f32[8]{0:T(128)S(1)}, f32[8]{0:T(128)}, u32[]{:S(2)}) copy-start(f32[8]{0:T(128)} %param.11) | copy-start | bytes 100
  62.3 1.2 %collective-permute-start = (f32[40]{0:T(128)S(1)}, f32[40]{0:T(128)S(1)}, u32[]{:S(2)}, u32[]{:S(2)}) collective-permute-start(f32[40]{0:T(128)S(1)} %multiply_reduce_fusion), channel_id=1, source_target_pairs={{0,1},{1,0},{2,3},{3,2},{4,5},{5,4},{6,7},{7,6},{8,9},{9,8},{10,11... | collective-permute-start | bytes 488 | tf_op jit(solution)/shard_map/ppermute | solution.py:44
  63.5 3.6 %collective-permute-start.1 = (f32[40]{0:T(128)S(1)}, f32[40]{0:T(128)S(1)}, u32[]{:S(2)}, u32[]{:S(2)}) collective-permute-start(f32[40]{0:T(128)S(1)} %add.85), channel_id=1, source_target_pairs={{0,2},{1,3},{2,0},{3,1},{4,6},{5,7},{6,4},{7,5},{8,10},{9,11},{10,... | collective-permute-start | bytes 488 | tf_op jit(solution)/shard_map/ppermute | solution.py:44
  67.1 4.5 %collective-permute-start.2 = (f32[40]{0:T(128)S(1)}, f32[40]{0:T(128)S(1)}, u32[]{:S(2)}, u32[]{:S(2)}) collective-permute-start(f32[40]{0:T(128)S(1)} %add.86), channel_id=1, source_target_pairs={{0,4},{1,5},{2,6},{3,7},{4,0},{5,1},{6,2},{7,3},{8,12},{9,13},{10,... | collective-permute-start | bytes 488 | tf_op jit(solution)/shard_map/ppermute | solution.py:44
  71.5 9.2 %copy-start.1 = (f32[40]{0:T(128)}, f32[40]{0:T(128)S(1)}, u32[]{:S(2)}) copy-start(f32[40]{0:T(128)S(1)} %add.87) | copy-start | bytes 484

commit v2 on v0

--- a/solution.py
+++ b/solution.py
@@ -41,7 +41,12 @@
     partial_sums = jnp.sum(jnp.sum(product, axis=2) * inverse, axis=0)
     couplings = lax.psum(partial_sums, "virt")
     local_sum = jnp.dot(first.T, couplings[:, None] * second, precision=lax.Precision.HIGHEST)
-    collected = lax.all_gather(local_sum[None], "pair", axis=0, tiled=True)
+    ring = [local_sum[None]]
+    for hop in range(3):
+        ring.append(lax.ppermute(ring[-1], "pair", [(dev, (dev + 1) % 4) for dev in range(4)]))
+    collected = jnp.roll(
+        jnp.concatenate(ring[::-1], axis=0), (lax.axis_index("pair") + 1) * ring[0].shape[0], axis=0
+    )
     coupling_sum = jnp.sum(collected, axis=0)
     heff = jnp.diag(state_energy) + 0.5 * (coupling_sum + coupling_sum.T)
     return (couplings, heff)

time: 83.2 us -> 90.7 us (1.090)
  waiting for transfers between devices: 0 us -> 11.4 us
  blocking collectives: 72.2 us -> 64.2 us
  starting transfers between devices: 0 us -> 2.08 us
  local copies, waits for them, and re-layouts: 3.48 us -> 5.46 us
    ppermute x0 -> x3, waiting for transfers between devices: none -> 11.4 us  [local(): lax.ppermute(ring[-1], 'pair', [(dev, (dev + 1) % 4) for dev in range(4)])]
    all_gather x1 -> x0, blocking collectives: 8.18 us -> none  [local(): collected = lax.all_gather(local_sum[None], 'pair', axis=0, tiled=True)]
    ppermute x0 -> x3, starting transfers between devices: none -> 2.08 us  [local(): lax.ppermute(ring[-1], 'pair', [(dev, (dev + 1) % 4) for dev in range(4)])]
    unnamed x15 -> x14, local copies, waits for them, and re-layouts: 0.89 us -> 2.12 us
  transfers between devices with their start and end apart: 0 -> 3, of which waited for: 0 -> 3; matrix products, arithmetic and copies ran while one was open for 0% -> 0% of each run, Pallas kernels for 0% -> 0%
where the time goes in v2:
time: 90.7 us; the launch traced here: 90.5 us
  blocking collectives  64.2 us (71%)
  waiting for transfers between devices  11.4 us (13%)
  local copies, waits for them, and re-layouts  5.46 us (6%)
  matrix products  4.29 us (5%)
  starting transfers between devices  2.08 us (2%)
  other arithmetic  1.57 us (2%)
  between operations  1.4 us (2%)
    unnamed x1, blocking collectives  17.7 us
    all_gather x1, blocking collectives, local(): lax.all_gather(vir_left, 'virt', axis=0, tiled=True)  17.2 us
    all_gather x1, blocking collectives, local(): right_piece = lax.all_gather(vir_right, 'virt', axis=0, tiled=True)  15.7 us
    psum x1, blocking collectives, local(): couplings = lax.psum(partial_sums, 'virt')  13.6 us
    ppermute x3, waiting for transfers between devices, local(): lax.ppermute(ring[-1], 'pair', [(dev, (dev + 1) % 4) for dev in range(4)])  11.4 us
    dot_general x1, matrix products, local(): lax.dot_general(right_piece, flat_rdm, (((1,), (1,)), ((), ())), preferre...  3.82 us
    unnamed x14, local copies, waits for them, and re-layouts  2.12 us
    ppermute x3, starting transfers between devices, local(): lax.ppermute(ring[-1], 'pair', [(dev, (dev + 1) % 4) for dev in range(4)])  2.08 us
  transfers between devices with their start and end apart: 3, of which 3 were waited for; matrix products, arithmetic and copies ran while one was open for 0% of the time, Pallas kernels for 0%

profile of v2, /device:TPU:0, one launch (start us, length us, event | category | flops | bytes accessed | tf_op | source)
XLA Modules:
  0.0 90.5 jit_solution(8254686450895379442)
XLA Ops:
  0.6 0.7 broadcast_add_fusion
  1.3 0.1 copy.22
  1.4 0.1 add.87
  1.5 17.2 %all_gather.9 = bf16[128,2744]{1,0:T(8,128)(2,1)S(1)} all-gather(bf16[16,2744]{1,0:T(8,128)(2,1)} %param.8), channel_id=1, replica_groups=mesh['pair'=4,'virt'=8] {'virt'}, dimensions={0}, use_global_device_ids=true | all-gather | bytes 790272 | tf_op jit(solution)/shard_map/all_gather | solution.py:28
  18.8 0.4 copy.23
  19.1 15.7 %all_gather.10 = bf16[128,2744]{1,0:T(8,128)(2,1)S(1)} all-gather(bf16[16,2744]{1,0:T(8,128)(2,1)} %param.9), channel_id=1, replica_groups=mesh['pair'=4,'virt'=8] {'virt'}, dimensions={0}, use_global_device_ids=true | all-gather | bytes 790272 | tf_op jit(solution)/shard_map/all_gather | solution.py:29
  34.8 0.8 slice_bitcast_fusion.1
  35.6 1.2 %dynamic-slice = u32[1]{0:T(128)} dynamic-slice(u32[32]{0:T(128)} %constant.60, u32[]{:T(128)S(6)} %add.96), dynamic_slice_sizes={1} | dynamic-slice | bytes 12
  37.5 0.9 dynamic-update-slice
  38.3 17.7 %all-reduce = bf16[128]{0:T(256)(128)(2,1)S(1)} all-reduce(bf16[128]{0:T(256)(128)(2,1)S(1)} %dynamic-update-slice), channel_id=1, replica_groups=mesh['pair'=4,'virt'=8] {'virt'}, use_global_device_ids=true, to_apply=%add | all-reduce | flops 128 | bytes 512
  56.0 2.0 %gather_fusion = bf16[640,128]{1,0:T(8,128)(2,1)S(1)} fusion(bf16[128,2744]{0,1:T(8,128)(2,1)S(1)} %copy.23, s32[1024]{0:T(1024)S(1)} %pad_clamp_fusion), kind=kCustom, calls=%fused_computation | custom fusion | bytes 330240 | tf_op jit(solution)/shard_map/jit(_take)/gather | solution.py:28
  58.0 0.2 convolution_bitcast_fusion.1
  58.2 3.8 %fusion.5 = f32[128,40]{0,1:T(8,128)S(1)} fusion(bf16[40,16,2744]{2,1,0:T(8,128)(2,1)} %param.7, bf16[128,2744]{1,0:T(8,128)(2,1)S(1)} %all_gather.10, bf16[128,40,16]{0,2,1:T(8,128)(2,1)S(1)} %bitcast.24, pred[40,16]{0,1:T(8,128)(4,1)S(1)} %compare_and_fusion), kind=kOutput, calls=%fused_computation.4 | convolution fusion | flops 449899520 | bytes 4399744 | tf_op jit(solution)/shard_map/dot_general | solution.py:31
  62.1 0.2 multiply_reduce_fusion
  62.3 13.6 %psum.7 = f32[40]{0:T(128)S(1)} all-reduce(f32[40]{0:T(128)S(1)} %multiply_reduce_fusion), channel_id=1, replica_groups=mesh['pair'=4,'virt'=8] {'virt'}, use_global_device_ids=true, to_apply=%region_2.3 | all-reduce | flops 40 | bytes 320 | tf_op jit(solution)/shard_map/psum | solution.py:42
  75.9 0.3 convolution_bitcast_fusion
  76.1 1.5 %collective-permute-start = (f32[1,8,8]{2,1,0:T(8,128)S(1)}, f32[1,8,8]{2,1,0:T(8,128)S(1)}, u32[]{:S(2)}, u32[]{:S(2)}) collective-permute-start(f32[1,8,8]{2,1,0:T(8,128)S(1)} %convolution_bitcast_fusion), channel_id=1, source_target_pairs={{0,8},{8,16},{16,24},{24,0},{1,9},{9,17},{17,25},{25,1},{2,10},{10... | collective-permute-start | bytes 776 | tf_op jit(solution)/shard_map/ppermute | solution.py:46
  77.6 3.0 %collective-permute-done = f32[1,8,8]{2,1,0:T(8,128)S(1)} collective-permute-done((f32[1,8,8]{2,1,0:T(8,128)S(1)}, f32[1,8,8]{2,1,0:T(8,128)S(1)}, u32[]{:S(2)}, u32[]{:S(2)}) %collective-permute-start) | collective-permute-done | bytes 288 | tf_op jit(solution)/shard_map/ppermute | solution.py:46
  80.6 0.6 collective-permute-start.1
  81.2 3.9 %collective-permute-done.1 = f32[1,8,8]{2,1,0:T(8,128)S(1)} collective-permute-done((f32[1,8,8]{2,1,0:T(8,128)S(1)}, f32[1,8,8]{2,1,0:T(8,128)S(1)}, u32[]{:S(2)}, u32[]{:S(2)}) %collective-permute-start.1) | collective-permute-done | bytes 288 | tf_op jit(solution)/shard_map/ppermute | solution.py:46
  85.1 0.0 collective-permute-start.2
  85.1 4.5 %collective-permute-done.2 = f32[1,8,8]{2,1,0:T(8,128)S(1)} collective-permute-done((f32[1,8,8]{2,1,0:T(8,128)S(1)}, f32[1,8,8]{2,1,0:T(8,128)S(1)}, u32[]{:S(2)}, u32[]{:S(2)}) %collective-permute-start.2) | collective-permute-done | bytes 288 | tf_op jit(solution)/shard_map/ppermute | solution.py:46
  89.7 0.1 copy.26
  89.8 0.7 fusion.20
  (19 shorter events, 0.1 us)
Async XLA Ops:
  0.6 57.4 %copy-start = (f32[8]{0:T(128)S(1)}, f32[8]{0:T(128)}, u32[]{:S(2)}) copy-start(f32[8]{0:T(128)} %param.11) | copy-start | bytes 100
  75.9 14.6 %copy-start.1 = (f32[40]{0:T(128)}, f32[40]{0:T(128)S(1)}, u32[]{:S(2)}) copy-start(f32[40]{0:T(128)S(1)} %psum.7) | copy-start | bytes 484
  76.1 4.5 %collective-permute-start = (f32[1,8,8]{2,1,0:T(8,128)S(1)}, f32[1,8,8]{2,1,0:T(8,128)S(1)}, u32[]{:S(2)}, u32[]{:S(2)}) collective-permute-start(f32[1,8,8]{2,1,0:T(8,128)S(1)} %convolution_bitcast_fusion), channel_id=1, source_target_pairs={{0,8},{8,16},{16,24},{24,0},{1,9},{9,17},{17,25},{25,1},{2,10},{10... | collective-permute-start | bytes 776 | tf_op jit(solution)/shard_map/ppermute | solution.py:46
  80.6 4.5 %collective-permute-start.1 = (f32[1,8,8]{2,1,0:T(8,128)S(1)}, f32[1,8,8]{2,1,0:T(8,128)S(1)}, u32[]{:S(2)}, u32[]{:S(2)}) collective-permute-start(f32[1,8,8]{2,1,0:T(8,128)S(1)} %collective-permute-done), channel_id=1, source_target_pairs={{0,8},{8,16},{16,24},{24,0},{1,9},{9,17},{17,25},{25,1},{2,10},{10... | collective-permute-start | bytes 776 | tf_op jit(solution)/shard_map/ppermute | solution.py:46
  85.1 4.5 %collective-permute-start.2 = (f32[1,8,8]{2,1,0:T(8,128)S(1)}, f32[1,8,8]{2,1,0:T(8,128)S(1)}, u32[]{:S(2)}, u32[]{:S(2)}) collective-permute-start(f32[1,8,8]{2,1,0:T(8,128)S(1)} %collective-permute-done.1), channel_id=1, source_target_pairs={{0,8},{8,16},{16,24},{24,0},{1,9},{9,17},{17,25},{25,1},{2,10},{10... | collective-permute-start | bytes 776 | tf_op jit(solution)/shard_map/ppermute | solution.py:46
